TPU v7x, 32 devices: a whole 2x2x4 slice. The times are simulated.
32 devices in a mesh: dp: 8 (over y, x, core), seq: 4 (over z).
Axes of the slice: x: 2, y: 2, z: 4, core: 2. Of those that a mesh axis runs over, the one named last changes fastest.
Arguments:
- block_input: bfloat16 [16, 512, 2048], P('dp', 'seq'), may hold values from -12 to 12
- segment_ids: int32 [16, 512], P('dp'), may hold values from 0 to 3, never falling along the last dimension, each value on 1 to 256 neighbouring positions
- cotangent: bfloat16 [16, 512, 2048], P('dp', 'seq'), may hold values from -6 to 6
- attn_gain: float32 [2048], P(('dp', 'seq')), may hold values from 0.5 to 1.5
- qkv_weight: float32 [2048, 3072], P('dp', 'seq'), may hold values from -1 to 1
- out_weight: float32 [2048, 2048], P('seq', 'dp'), may hold values from -0.75 to 0.75
- mlp_gain: float32 [2048], P(('dp', 'seq')), may hold values from 0.5 to 1.5
- gate_up_weight: float32 [2048, 2, 8192], P('dp', None, 'seq'), may hold values from -0.125 to 0.125
- down_weight: float32 [8192, 2048], P('seq', 'dp'), may hold values from -0.125 to 0.125
- first_attn_gain: float32 [2048], P(('dp', 'seq')), may hold values from -30 to 30
- first_qkv: float32 [2048, 3072], P('dp', 'seq'), may hold values from -30 to 30
- first_out: float32 [2048, 2048], P('seq', 'dp'), may hold values from -30 to 30
- first_mlp_gain: float32 [2048], P(('dp', 'seq')), may hold values from -30 to 30
- first_gate_up: float32 [2048, 2, 8192], P('dp', None, 'seq'), may hold values from -30 to 30
- first_down: float32 [8192, 2048], P('seq', 'dp'), may hold values from -30 to 30
- second_attn_gain: float32 [2048], P(('dp', 'seq')), may hold values from 100 to 300000
- second_qkv: float32 [2048, 3072], P('dp', 'seq'), may hold values from 100 to 30000
- second_out: float32 [2048, 2048], P('seq', 'dp'), may hold values from 50 to 500
- second_mlp_gain: float32 [2048], P(('dp', 'seq')), may hold values from 50 to 500
- second_gate_up: float32 [2048, 2, 8192], P('dp', None, 'seq'), may hold values from 50 to 500
- second_down: float32 [8192, 2048], P('seq', 'dp'), may hold values from 50 to 500
Outputs:
- output: bfloat16 [16, 512, 2048], P('dp', 'seq')
- input_grad: bfloat16 [16, 512, 2048], P('dp', 'seq')
- grad_attn_gain: float32 [2048], P(('dp', 'seq'))
- grad_qkv: float32 [2048, 3072], P('dp', 'seq')
- grad_out: float32 [2048, 2048], P('seq', 'dp')
- grad_mlp_gain: float32 [2048], P(('dp', 'seq'))
- grad_gate_up: float32 [2048, 2, 8192], P('dp', None, 'seq')
- grad_down: float32 [8192, 2048], P('seq', 'dp')
- new_attn_gain: float32 [2048], P(('dp', 'seq'))
- new_qkv: float32 [2048, 3072], P('dp', 'seq')
- new_out: float32 [2048, 2048], P('seq', 'dp')
- new_mlp_gain: float32 [2048], P(('dp', 'seq'))
- new_gate_up: float32 [2048, 2, 8192], P('dp', None, 'seq')
- new_down: float32 [8192, 2048], P('seq', 'dp')
- new_first_attn_gain: float32 [2048], P(('dp', 'seq'))
- new_first_qkv: float32 [2048, 3072], P('dp', 'seq')
- new_first_out: float32 [2048, 2048], P('seq', 'dp')
- new_first_mlp_gain: float32 [2048], P(('dp', 'seq'))
- new_first_gate_up: float32 [2048, 2, 8192], P('dp', None, 'seq')
- new_first_down: float32 [8192, 2048], P('seq', 'dp')
- new_second_attn_gain: float32 [2048], P(('dp', 'seq'))
- new_second_qkv: float32 [2048, 3072], P('dp', 'seq')
- new_second_out: float32 [2048, 2048], P('seq', 'dp')
- new_second_mlp_gain: float32 [2048], P(('dp', 'seq'))
- new_second_gate_up: float32 [2048, 2, 8192], P('dp', None, 'seq')
- new_second_down: float32 [8192, 2048], P('seq', 'dp')
Inputs may be any that keep to these rules, and one draw needn't show every extreme that they name: `segment_ids`: in each sequence the numbers never fall, and each segment holds 1 to 256 consecutive positions, one of them exactly that many.
All inputs are finite; a program needn't handle non-finite values.
Results may differ from a plain program's by a relative error of at most 0.023.
Values may be sent and summed in bfloat16 or wider, within the bound.
A program may use at most 320 MiB of HBM per device.

v0:
```python
import jax
import jax.numpy as jnp
from jax import lax
from jax.sharding import PartitionSpec as P

HEADS = 32
KV_HEADS = 8
HEAD_DIM = 64
norm_eps = 1e-05
rope_base = 500000.0
beta_one = 0.9
beta_two = 0.95
learn_rate = 0.01
weight_decay = 0.1
adam_eps = 1e-08
step_count = 10.0
masked_score = -1e30


def segment_positions(segments):
    length_here = segments.shape[-1]
    earlier = (segments[..., None, :] < segments[..., :, None]).astype(jnp.int32)
    return jnp.arange(length_here, dtype=jnp.int32) - jnp.sum(earlier, axis=-1, dtype=jnp.int32)


def rope_tables(positions, head_size):
    half_size = head_size // 2
    inverse = rope_base ** (-2.0 * jnp.arange(half_size, dtype=jnp.float32) / head_size)
    angles = positions.astype(jnp.float32)[..., None] * inverse
    return (jnp.cos(angles), jnp.sin(angles))


def rotate(vectors, cosine, sine):
    half_size = vectors.shape[-1] // 2
    first_half = vectors[..., :half_size]
    second_half = vectors[..., half_size:]
    cos_wide = cosine[..., None, :]
    sin_wide = sine[..., None, :]
    return jnp.concatenate(
        [
            first_half * cos_wide - second_half * sin_wide,
            second_half * cos_wide + first_half * sin_wide,
        ],
        -1,
    )


def unrotate(vectors, cosine, sine):
    half_size = vectors.shape[-1] // 2
    first_half = vectors[..., :half_size]
    second_half = vectors[..., half_size:]
    cos_wide = cosine[..., None, :]
    sin_wide = sine[..., None, :]
    return jnp.concatenate(
        [
            first_half * cos_wide + second_half * sin_wide,
            second_half * cos_wide - first_half * sin_wide,
        ],
        -1,
    )


def rms_forward(values, gain_wide):
    inverse = lax.rsqrt(jnp.mean(values * values, axis=-1, keepdims=True) + norm_eps)
    scaled = values * inverse
    return (scaled, inverse, (scaled * gain_wide).astype(jnp.bfloat16))


def rms_backward(d_normed, scaled, inverse, gain_wide):
    d_scaled = d_normed * gain_wide
    d_values = inverse * (d_scaled - scaled * jnp.mean(d_scaled * scaled, axis=-1, keepdims=True))
    return (d_values, jnp.sum(d_normed * scaled, axis=0))


def adam_update(weight, grad, first, second):
    new_first = beta_one * first + (1.0 - beta_one) * grad
    new_second = beta_two * second + (1.0 - beta_two) * grad * grad
    first_hat = new_first / (1.0 - beta_one**step_count)
    second_hat = new_second / (1.0 - beta_two**step_count)
    new_weight = weight - learn_rate * (
        first_hat / (jnp.sqrt(second_hat) + adam_eps) + weight_decay * weight
    )
    return (new_weight, new_first, new_second)


def contract_rows(left, right):
    return lax.dot_general(
        left, right, (((0,), (0,)), ((), ())), preferred_element_type=jnp.float32
    )


def times_transpose(left, right):
    return lax.dot_general(
        left, right, (((1,), (1,)), ((), ())), preferred_element_type=jnp.float32
    )


def per_device(
    block_input,
    segment_ids,
    cotangent,
    attn_gain,
    qkv_weight,
    out_weight,
    mlp_gain,
    gate_up_weight,
    down_weight,
    first_attn_gain,
    first_qkv,
    first_out,
    first_mlp_gain,
    first_gate_up,
    first_down,
    second_attn_gain,
    second_qkv,
    second_out,
    second_mlp_gain,
    second_gate_up,
    second_down,
):
    seqs_here, local_len, width = block_input.shape
    full_len = segment_ids.shape[1]
    total_rows = seqs_here * full_len
    groups = HEADS // KV_HEADS
    slot_count = groups + 2
    kv_local = qkv_weight.shape[1] // (slot_count * HEAD_DIM)
    query_cols = kv_local * groups * HEAD_DIM
    unit_count = down_weight.shape[0]
    score_scale = HEAD_DIM ** (-0.5)
    local_rows = seqs_here * local_len
    gain_pair = jnp.stack([attn_gain, mlp_gain]).astype(jnp.bfloat16)
    gain_block = lax.all_gather(gain_pair, ("dp", "seq"), axis=1, tiled=True)
    gain_one = gain_block[0].astype(jnp.float32)
    gain_two = gain_block[1].astype(jnp.float32)
    local_input = block_input.reshape(local_rows, width).astype(jnp.float32)
    scaled_one, inverse_one, normed_here = rms_forward(local_input, gain_one)
    normed_one = lax.all_gather(
        normed_here.reshape(seqs_here, local_len, width), "seq", axis=1, tiled=True
    ).reshape(total_rows, width)
    qkv_cols = lax.all_gather(qkv_weight.astype(jnp.bfloat16), "dp", axis=0, tiled=True)
    out_rows = lax.all_gather(out_weight.astype(jnp.bfloat16), "dp", axis=1, tiled=True)
    gate_up_cols = lax.all_gather(
        gate_up_weight.astype(jnp.bfloat16).reshape(-1, 2 * unit_count), "dp", axis=0, tiled=True
    )
    cot_all = lax.all_gather(cotangent, "seq", axis=1, tiled=True)
    down_rows = lax.all_gather(down_weight.astype(jnp.bfloat16), "dp", axis=1, tiled=True)
    positions = segment_positions(segment_ids)
    cosine, sine = rope_tables(positions, HEAD_DIM)
    index_line = jnp.arange(full_len, dtype=jnp.int32)
    allowed = (segment_ids[:, :, None] == segment_ids[:, None, :]) & (
        index_line[None, None, :] <= index_line[None, :, None]
    )
    allowed = allowed[:, None, None, :, :]
    qkv = jnp.dot(normed_one, qkv_cols, preferred_element_type=jnp.float32)
    qkv = qkv.reshape(seqs_here, full_len, kv_local, slot_count, HEAD_DIM)
    query = qkv[:, :, :, :groups].reshape(seqs_here, full_len, kv_local * groups, HEAD_DIM)
    query_groups = (
        rotate(query, cosine, sine)
        .astype(jnp.bfloat16)
        .reshape(seqs_here, full_len, kv_local, groups, HEAD_DIM)
    )
    key16 = rotate(qkv[:, :, :, groups], cosine, sine).astype(jnp.bfloat16)
    value16 = qkv[:, :, :, groups + 1].astype(jnp.bfloat16)

    def masked_scores():
        raw_scores = (
            jnp.einsum("sqgjd,skgd->sgjqk", query_groups, key16, preferred_element_type=jnp.float32)
            * score_scale
        )
        return jnp.where(allowed, raw_scores, masked_score)

    scores = masked_scores()
    top_score = jnp.max(scores, axis=-1, keepdims=True)
    log_total = top_score + jnp.log(jnp.sum(jnp.exp(scores - top_score), axis=-1, keepdims=True))
    probs16 = jnp.exp(scores - log_total).astype(jnp.bfloat16)
    attended16 = jnp.einsum(
        "sgjqk,skgd->sqgjd", probs16, value16, preferred_element_type=jnp.float32
    )
    attended16 = attended16.reshape(total_rows, query_cols).astype(jnp.bfloat16)
    attn_part = jnp.dot(attended16, out_rows, preferred_element_type=jnp.float32)

    def to_local(part):
        return (
            lax.psum_scatter(
                part.astype(jnp.bfloat16).reshape(seqs_here, full_len, width),
                "seq",
                scatter_dimension=1,
                tiled=True,
            )
            .astype(jnp.float32)
            .reshape(local_rows, width)
        )

    resid = local_input + to_local(attn_part)
    scaled_two, inverse_two, normed_two_here = rms_forward(resid, gain_two)
    normed_two = lax.all_gather(
        normed_two_here.reshape(seqs_here, local_len, width), "seq", axis=1, tiled=True
    ).reshape(total_rows, width)
    gate_up = jnp.dot(normed_two, gate_up_cols, preferred_element_type=jnp.float32)
    gate_part = gate_up[:, :unit_count]
    up_part = gate_up[:, unit_count:]
    sigmoid_gate = jax.nn.sigmoid(gate_part)
    active = gate_part * sigmoid_gate
    hidden16 = (active * up_part).astype(jnp.bfloat16)
    down_part = jnp.dot(hidden16, down_rows, preferred_element_type=jnp.float32)
    output = (resid + to_local(down_part)).astype(jnp.bfloat16).reshape(block_input.shape)
    cot_rows = cot_all.reshape(total_rows, width)
    d_hidden = times_transpose(cot_rows, down_rows)
    d_gate = d_hidden * up_part * sigmoid_gate * (1.0 + gate_part * (1.0 - sigmoid_gate))
    d_up = d_hidden * active
    d_gate_up16 = jnp.concatenate([d_gate, d_up], 1).astype(jnp.bfloat16)
    d_normed_two = to_local(times_transpose(d_gate_up16, gate_up_cols))
    down_term = contract_rows(cot_rows, hidden16)
    gate_up_term = contract_rows(normed_two, d_gate_up16)
    down_sum = lax.psum_scatter(
        down_term.astype(jnp.bfloat16), "dp", scatter_dimension=0, tiled=True
    ).astype(jnp.float32)
    grad_gate_up = (
        lax.psum_scatter(gate_up_term.astype(jnp.bfloat16), "dp", scatter_dimension=0, tiled=True)
        .reshape(gate_up_weight.shape)
        .astype(jnp.float32)
    )
    grad_down = down_sum.T
    resid_part, gain_two_term = rms_backward(d_normed_two, scaled_two, inverse_two, gain_two)
    d_resid = cotangent.reshape(local_rows, width).astype(jnp.float32) + resid_part
    d_resid16 = lax.all_gather(
        d_resid.astype(jnp.bfloat16).reshape(seqs_here, local_len, width), "seq", axis=1, tiled=True
    ).reshape(total_rows, width)
    d_attended = times_transpose(d_resid16, out_rows).astype(jnp.bfloat16)
    d_attended = d_attended.reshape(seqs_here, full_len, kv_local, groups, HEAD_DIM)
    scores = masked_scores()
    probs = jnp.exp(scores - log_total)
    d_probs = jnp.einsum(
        "sqgjd,skgd->sgjqk", d_attended, value16, preferred_element_type=jnp.float32
    )
    delta = jnp.sum(probs * d_probs, axis=-1, keepdims=True)
    d_scores16 = (probs * (d_probs - delta) * score_scale).astype(jnp.bfloat16)
    d_query = jnp.einsum("sgjqk,skgd->sqgjd", d_scores16, key16, preferred_element_type=jnp.float32)
    d_key = jnp.einsum(
        "sgjqk,sqgjd->skgd", d_scores16, query_groups, preferred_element_type=jnp.float32
    )
    d_value = jnp.einsum(
        "sgjqk,sqgjd->skgd", probs16, d_attended, preferred_element_type=jnp.float32
    )
    d_query = unrotate(
        d_query.reshape(seqs_here, full_len, kv_local * groups, HEAD_DIM), cosine, sine
    )
    d_query = d_query.reshape(seqs_here, full_len, kv_local, groups, HEAD_DIM)
    d_key = unrotate(d_key, cosine, sine)
    d_qkv16 = jnp.concatenate([d_query, d_key[:, :, :, None], d_value[:, :, :, None]], 3)
    d_qkv16 = d_qkv16.reshape(total_rows, qkv_cols.shape[1]).astype(jnp.bfloat16)
    d_normed_one = to_local(times_transpose(d_qkv16, qkv_cols))
    qkv_term = contract_rows(normed_one, d_qkv16)
    out_term = contract_rows(d_resid16, attended16)
    grad_qkv = lax.psum_scatter(
        qkv_term.astype(jnp.bfloat16), "dp", scatter_dimension=0, tiled=True
    ).astype(jnp.float32)
    out_sum = lax.psum_scatter(
        out_term.astype(jnp.bfloat16), "dp", scatter_dimension=0, tiled=True
    ).astype(jnp.float32)
    grad_out = out_sum.T
    input_part, gain_one_term = rms_backward(d_normed_one, scaled_one, inverse_one, gain_one)
    input_grad = (d_resid + input_part).astype(jnp.bfloat16).reshape(block_input.shape)
    gain_grads = lax.psum_scatter(
        jnp.stack([gain_one_term, gain_two_term], 1), ("dp", "seq"), scatter_dimension=0, tiled=True
    )
    grad_gain_one = gain_grads[:, 0]
    grad_gain_two = gain_grads[:, 1]
    w_one, m_one, v_one = adam_update(attn_gain, grad_gain_one, first_attn_gain, second_attn_gain)
    w_qkv, m_qkv, v_qkv = adam_update(qkv_weight, grad_qkv, first_qkv, second_qkv)
    w_out, m_out, v_out = adam_update(out_weight, grad_out, first_out, second_out)
    w_two, m_two, v_two = adam_update(mlp_gain, grad_gain_two, first_mlp_gain, second_mlp_gain)
    w_gu, m_gu, v_gu = adam_update(gate_up_weight, grad_gate_up, first_gate_up, second_gate_up)
    w_down, m_down, v_down = adam_update(down_weight, grad_down, first_down, second_down)
    return (
        output,
        input_grad,
        grad_gain_one,
        grad_qkv,
        grad_out,
        grad_gain_two,
        grad_gate_up,
        grad_down,
        w_one,
        w_qkv,
        w_out,
        w_two,
        w_gu,
        w_down,
        m_one,
        m_qkv,
        m_out,
        m_two,
        m_gu,
        m_down,
        v_one,
        v_qkv,
        v_out,
        v_two,
        v_gu,
        v_down,
    )


def solution(mesh):
    in_specs = (
        P("dp", "seq", None),
        P("dp", None),
        P("dp", "seq", None),
        P(("dp", "seq")),
        P("dp", "seq"),
        P("seq", "dp"),
        P(("dp", "seq")),
        P("dp", None, "seq"),
        P("seq", "dp"),
        P(("dp", "seq")),
        P("dp", "seq"),
        P("seq", "dp"),
        P(("dp", "seq")),
        P("dp", None, "seq"),
        P("seq", "dp"),
        P(("dp", "seq")),
        P("dp", "seq"),
        P("seq", "dp"),
        P(("dp", "seq")),
        P("dp", None, "seq"),
        P("seq", "dp"),
    )
    out_specs = (
        P("dp", "seq", None),
        P("dp", "seq", None),
        P(("dp", "seq")),
        P("dp", "seq"),
        P("seq", "dp"),
        P(("dp", "seq")),
        P("dp", None, "seq"),
        P("seq", "dp"),
        P(("dp", "seq")),
        P("dp", "seq"),
        P("seq", "dp"),
        P(("dp", "seq")),
        P("dp", None, "seq"),
        P("seq", "dp"),
        P(("dp", "seq")),
        P("dp", "seq"),
        P("seq", "dp"),
        P(("dp", "seq")),
        P("dp", None, "seq"),
        P("seq", "dp"),
        P(("dp", "seq")),
        P("dp", "seq"),
        P("seq", "dp"),
        P(("dp", "seq")),
        P("dp", None, "seq"),
        P("seq", "dp"),
    )
    return jax.shard_map(
        per_device, mesh=mesh, in_specs=in_specs, out_specs=out_specs, check_vma=False
    )
```

profile of v0, /device:TPU:0, one launch (start us, length us, event | category | flops | bytes accessed | tf_op | source)
XLA Modules:
  0.0 1514.0 jit_solution(13102967327842110868)
XLA Ops:
  7.3 2.0 convert_element_type.162
  10.0 69.8 %all-gather = bf16[32,64,2]{1,2,0:T(2,128)(2,1)S(1)} all-gather(bf16[1,64,2]{1,2,0:T(2,128)(2,1)S(1)} %maximum_bitcast_fusion.4), channel_id=1, replica_groups=mesh['dp'=8,'seq'=4] {'dp','seq'}, dimensions={0}, use_global_device_ids=true | all-gather | bytes 8448 | tf_op jit(solution)/shard_map/all_gather | solution.py:132
  79.9 1.5 fusion.32
  81.5 2.5 fusion.29
  86.3 4.8 copy.86
  91.1 70.0 %all-gather.10.cloned.1.call-done = bf16[2,512,2048]{2,1,0:T(8,128)(2,1)} async-done(((bf16[2,128,2048]{2,1,0:T(8,128)(2,1)}), bf16[2,512,2048]{2,1,0:T(8,128)(2,1)}) %all-gather.10.cloned.1.call-update) | async-done | bytes 4194320 | tf_op jit(solution)/shard_map/all_gather | solution.py:137
  161.2 6.3 fusion.9
  169.2 7.4 fusion.5
  176.6 9.6 exponential_reduce_fusion
  186.2 10.3 fusion.35
  196.5 1.1 copy.88
  197.9 6.4 convolution_convert_fusion.2
  204.3 75.1 %reduce-scatter.12.cloned.1.call-done = bf16[2,128,2048]{2,1,0:T(8,128)(2,1)} async-done(((bf16[2,512,2048]{2,1,0:T(8,128)(2,1)}), bf16[2,128,2048]{2,1,0:T(8,128)(2,1)}) %reduce-scatter.12.cloned.1.call-update) | async-done | bytes 1048592 | tf_op jit(solution)/shard_map/reduce_scatter | solution.py:184
  279.4 1.6 multiply_reduce_fusion
  281.0 2.6 multiply_convert_fusion.3
  283.7 4.2 convert_element_type.174
  287.9 2.2 copy.122
  292.1 72.9 %all-gather.16.cloned.1.call-done = bf16[2,512,2048]{2,1,0:T(8,128)(2,1)} async-done(((bf16[2,128,2048]{2,1,0:T(8,128)(2,1)}), bf16[2,512,2048]{2,1,0:T(8,128)(2,1)}) %all-gather.16.cloned.1.call-update) | async-done | bytes 4194320 | tf_op jit(solution)/shard_map/all_gather | solution.py:196
  365.0 90.6 %all-gather.18.cloned.1.call-done = bf16[2048,4096]{1,0:T(8,128)(2,1)} async-done(((bf16[256,4096]{1,0:T(8,128)(2,1)}), bf16[2048,4096]{1,0:T(8,128)(2,1)}) %all-gather.18.cloned.1.call-update) | async-done | bytes 16777232 | tf_op jit(solution)/shard_map/all_gather | solution.py:142
  455.6 23.9 %fusion.71 = f32[1024,4096]{1,0:T(8,128)} fusion(bf16[1024,2048]{1,0:T(8,128)(2,1)} %bitcast.221, bf16[2048,4096]{1,0:T(8,128)(2,1)} %all-gather.18.cloned.1.call-done), kind=kOutput, calls=%fused_computation.139 | convolution fusion | flops 17179869184 | bytes 37748736 | tf_op jit(solution)/shard_map/dot_general | solution.py:199
  479.5 58.4 %all-gather.22.cloned.1.call-done = bf16[2,512,2048]{2,1,0:T(8,128)(2,1)} async-done(((bf16[2,128,2048]{2,1,0:T(8,128)(2,1)}), bf16[2,512,2048]{2,1,0:T(8,128)(2,1)}) %all-gather.22.cloned.1.call-update) | async-done | bytes 4194320 | tf_op jit(solution)/shard_map/all_gather | solution.py:145
  538.0 56.8 %all-gather.20.cloned.1.call-done = bf16[2048,2048]{1,0:T(8,128)(2,1)} async-done(((bf16[2048,256]{1,0:T(8,128)(2,1)}), bf16[2048,2048]{1,0:T(8,128)(2,1)}) %all-gather.20.cloned.1.call-update) | async-done | bytes 8388624 | tf_op jit(solution)/shard_map/all_gather | solution.py:146
  594.8 21.7 %multiply_convert_fusion.1 = (bf16[1024,2048]{1,0:T(8,128)(2,1)}, bf16[1024,2048]{1,0:T(8,128)(2,1)}, bf16[1024,2048]{1,0:T(8,128)(2,1)}) fusion(f32[1024,4096]{1,0:T(8,128)} %fusion.71, bf16[1024,2048]{1,0:T(8,128)(2,1)} %bitcast.223, bf16[2048,2048]{1,0:T(8,128)(2,1)} %all-gather.20.cloned.1.call-done), kind=kOutput, calls=%fused_computation.15 | convolution fusion | flops 8621391872 | bytes 41943040 | tf_op jit(solution)/shard_map/dot_general | solution.py:93
  616.5 23.8 %fusion.11 = bf16[1024,2048]{1,0:T(8,128)(2,1)} fusion(bf16[2048,4096]{1,0:T(8,128)(2,1)} %all-gather.18.cloned.1.call-done, bf16[1024,2048]{1,0:T(8,128)(2,1)} %get-tuple-element.129, bf16[1024,2048]{1,0:T(8,128)(2,1)} %get-tuple-element.128), kind=kOutput, calls=%fused_computation.26 | convolution fusion | flops 17198743552 | bytes 29360128 | tf_op jit(solution)/shard_map/dot_general | solution.py:93
  640.6 76.7 %reduce-scatter.16.cloned.1.call-done = bf16[2,128,2048]{2,1,0:T(8,128)(2,1)} async-done(((bf16[2,512,2048]{2,1,0:T(8,128)(2,1)}), bf16[2,128,2048]{2,1,0:T(8,128)(2,1)}) %reduce-scatter.16.cloned.1.call-update) | async-done | bytes 1048592 | tf_op jit(solution)/shard_map/reduce_scatter | solution.py:184
  717.3 2.0 fusion.28
  719.4 3.2 fusion.38
  722.7 81.3 %all-gather.24.cloned.1.call-done = bf16[2,512,2048]{2,1,0:T(8,128)(2,1)} async-done(((bf16[2,128,2048]{2,1,0:T(8,128)(2,1)}), bf16[2,512,2048]{2,1,0:T(8,128)(2,1)}) %all-gather.24.cloned.1.call-update) | async-done | bytes 4194320 | tf_op jit(solution)/shard_map/all_gather | solution.py:226
  804.0 6.2 convolution_convert_fusion.7
  810.2 4.6 reshape.347
  814.8 4.0 copy.90
  818.9 9.5 fusion.42
  828.4 24.6 %fusion.18 = f32[2,2,64,4,512]{4,2,3,1,0:T(8,128)} fusion(f32[2,2,512,512,4]{3,2,4,1,0:T(8,128)} %fusion.42, f32[2,2,512,512,4]{3,2,4,1,0:T(8,128)} %get-tuple-element.148, f32[2,2,4,512]{3,2,1,0:T(4,128)S(1)} %bitcast.215, pred[2,512,512]{1,2,0:T(8,128)(4,1)} %copy-done.10, bf16[2,512,2,32]{1,3,2,0:T(8,128)(2,1)S(1)} %get-tuple-element.140, ...), kind=kOutput, calls=%fused_computation.42 | convolution fusion | flops 583541248 | bytes 36470784 | tf_op jit(solution)/shard_map/sgjqk,skgd->sqgjd/dot_general | solution.py:238
  853.0 24.9 %fusion.36 = f32[2,512,2,64]{1,3,2,0:T(8,128)} fusion(f32[2,2,512,512,4]{3,2,4,1,0:T(8,128)} %fusion.42, f32[2,2,512,512,4]{3,2,4,1,0:T(8,128)} %get-tuple-element.148, f32[2,2,4,512]{3,2,1,0:T(4,128)S(1)} %bitcast.216, pred[2,512,512]{1,2,0:T(8,128)(4,1)} %copy-done.10, bf16[2,512,2,4,32]{1,4,3,2,0:T(8,128)(2,1)} %bitcast.201, ...), kind=kOutput, calls=%fused_computation.75 | convolution fusion | flops 585114112 | bytes 35684352 | tf_op jit(solution)/shard_map/sgjqk,sqgjd->skgd/dot_general | solution.py:239
  877.9 10.3 convolution_bitcast_fusion
  890.5 6.1 maximum_convert_fusion
  897.1 5.0 convolution_convert_fusion.3
  902.2 14.5 convert_bitcast_fusion
  916.8 6.2 convolution_convert_fusion.5
  923.1 7.9 convolution_convert_fusion.4
  931.1 14.0 convolution_convert_fusion.1
  945.2 32.4 %reduce-scatter.18.cloned.1.call-done = bf16[2,128,2048]{2,1,0:T(8,128)(2,1)} async-done(((bf16[2,512,2048]{2,1,0:T(8,128)(2,1)}), bf16[2,128,2048]{2,1,0:T(8,128)(2,1)}) %reduce-scatter.18.cloned.1.call-update) | async-done | bytes 1048592 | tf_op jit(solution)/shard_map/reduce_scatter | solution.py:184
  977.6 1.9 fusion.31
  979.6 1.3 copy.115
  981.0 25.4 %convolution_convert_fusion = bf16[2048,4096]{1,0:T(8,128)(2,1)} fusion(bf16[1024,2048]{1,0:T(8,128)(2,1)} %bitcast.222, bf16[1024,2048]{1,0:T(8,128)(2,1)} %get-tuple-element.129, bf16[1024,2048]{1,0:T(8,128)(2,1)} %get-tuple-element.128), kind=kOutput, calls=%fused_computation.9 | convolution fusion | flops 17205035008 | bytes 29360128 | tf_op jit(solution)/shard_map/dot_general | solution.py:87
  1006.4 2.2 copy.101
  1008.6 2.0 copy.98
  1010.7 2.0 copy.99
  1012.7 40.1 %reduce-scatter.26.cloned.1.call-done = bf16[256,2048]{0,1:T(8,128)(2,1)} async-done(((bf16[2048,2048]{0,1:T(8,128)(2,1)}), bf16[256,2048]{0,1:T(8,128)(2,1)}) %reduce-scatter.26.cloned.1.call-update) | async-done | bytes 1048592 | tf_op jit(solution)/shard_map/reduce_scatter | solution.py:215
  1052.8 6.9 multiply_subtract_fusion.1
  1059.6 37.5 %reduce-scatter.22.cloned.1.call-done = bf16[256,512]{1,0:T(8,128)(2,1)} async-done(((bf16[2048,512]{1,0:T(8,128)(2,1)}), bf16[256,512]{1,0:T(8,128)(2,1)}) %reduce-scatter.22.cloned.1.call-update) | async-done | bytes 262160 | tf_op jit(solution)/shard_map/reduce_scatter | solution.py:258
  1097.2 2.9 multiply_subtract_fusion.4
  1100.1 2.0 copy.103
  1102.1 2.0 copy.104
  1104.2 2.0 copy.105
  1107.0 2.1 copy.102
  1109.1 37.4 %reduce-scatter.20.cloned.1.call-done = bf16[256,768]{1,0:T(8,128)(2,1)} async-done(((bf16[2048,768]{1,0:T(8,128)(2,1)}), bf16[256,768]{1,0:T(8,128)(2,1)}) %reduce-scatter.20.cloned.1.call-update) | async-done | bytes 393232 | tf_op jit(solution)/shard_map/reduce_scatter | solution.py:255
  1146.5 3.5 multiply_subtract_fusion.3
  1150.1 75.4 %reduce-scatter.14.cloned.1.call-done = bf16[2,128,2048]{2,1,0:T(8,128)(2,1)} async-done(((bf16[2,512,2048]{2,1,0:T(8,128)(2,1)}), bf16[2,128,2048]{2,1,0:T(8,128)(2,1)}) %reduce-scatter.14.cloned.1.call-update) | async-done | bytes 1048592 | tf_op jit(solution)/shard_map/reduce_scatter | solution.py:184
  1225.5 4.9 fusion.24
  1230.4 135.3 %reduce-scatter.28.cloned.1.call-done = f32[64,2]{1,0:T(8,128)} async-done(((f32[2048,2]{1,0:T(8,128)}), f32[64,2]{1,0:T(8,128)}) %reduce-scatter.28.cloned.1.call-update) | async-done | bytes 528
  1367.9 113.8 %reduce-scatter.24.cloned.1.call-done = bf16[256,4096]{1,0:T(8,128)(2,1)} async-done(((bf16[2048,4096]{1,0:T(8,128)(2,1)}), bf16[256,4096]{1,0:T(8,128)(2,1)}) %reduce-scatter.24.cloned.1.call-update) | async-done | bytes 2097168 | tf_op jit(solution)/shard_map/reduce_scatter | solution.py:219
  1481.7 6.6 reshape.336
  1488.3 18.9 %multiply_subtract_fusion = (f32[256,2,2048]{2,1,0:T(2,128)}, f32[256,2,2048]{2,1,0:T(2,128)}, f32[256,2,2048]{2,1,0:T(2,128)}) fusion(f32[256,2,2048]{2,1,0:T(2,128)} %param.28, f32[256,2,2048]{2,1,0:T(2,128)} %reshape.336, f32[256,2,2048]{2,1,0:T(2,128)} %param.34, f32[256,2,2048]{2,1,0:T(2,128)} %param.40), kind=kLoop, calls=%fused_computation.24 | loop fusion | flops 15728640 | bytes 29360128 | tf_op jit(solution)/shard_map/sub | solution.py:80
  (138 shorter events, 13.5 us)
Async XLA Ops:
  7.2 76.8 %copy-start.11 = (f32[512,256]{1,0:T(8,128)S(1)}, f32[512,256]{1,0:T(8,128)}, u32[]{:S(2)}) copy-start(f32[512,256]{1,0:T(8,128)} %param.26) | copy-start | bytes 1572868
  7.2 77.8 %copy-start.21 = (s32[2,512]{1,0:T(2,128)S(1)}, s32[2,512]{1,0:T(2,128)}, u32[]{:S(2)}) copy-start(s32[2,512]{1,0:T(2,128)} %param.22) | copy-start | bytes 12292
  7.2 79.1 %all-gather.12.cloned.1.call-start = ((), (), s32[]{:S(2)}) async-start(), calls=%async_computation.10 | async-start | bytes 3538944 | tf_op jit(solution)/shard_map/all_gather | solution.py:140
  9.3 151.9 %all-gather.10.cloned.1.call-start = ((), (), s32[]{:S(2)}) async-start(), calls=%async_computation.9 | async-start | bytes 5242880 | tf_op jit(solution)/shard_map/all_gather | solution.py:137
  81.4 3.8 copy-start.22
  81.5 3.8 copy-start.19
  84.0 113.9 %all-gather.14.cloned.1.call-start = ((), (), s32[]{:S(2)}) async-start(), calls=%async_computation.11 | async-start | bytes 2359296 | tf_op jit(solution)/shard_map/all_gather | solution.py:141
  84.8 194.6 %reduce-scatter.12.cloned.1.call-start = ((), (), s32[]{:S(2)}) async-start(), calls=%async_computation.12 | async-start | bytes 5242880 | tf_op jit(solution)/shard_map/reduce_scatter | solution.py:184
  85.7 100.4 %copy-start.10 = (pred[2,512,512]{1,2,0:T(8,128)(4,1)}, pred[2,512,512]{1,2,0:T(8,128)(4,1)S(1)}, u32[]{:S(2)}) copy-start(pred[2,512,512]{1,2,0:T(8,128)(4,1)S(1)} %compare_and_fusion) | copy-start | bytes 1572868
  86.3 81.5 %copy-start.4 = (f32[2,512,32]{1,2,0:T(8,128)}, f32[2,512,32]{1,2,0:T(8,128)S(1)}, u32[]{:S(2)}) copy-start(f32[2,512,32]{1,2,0:T(8,128)S(1)} %get-tuple-element.145) | copy-start | bytes 393220
  86.3 81.5 %copy-start.6 = (f32[2,512,32]{1,2,0:T(8,128)}, f32[2,512,32]{1,2,0:T(8,128)S(1)}, u32[]{:S(2)}) copy-start(f32[2,512,32]{1,2,0:T(8,128)S(1)} %get-tuple-element.146) | copy-start | bytes 393220
  167.5 1.7 copy-start.9
  169.2 7.4 copy-start.17
  169.2 7.4 copy-start.18
  197.9 6.4 copy-start.14
  204.2 75.1 %copy-start = (bf16[2,128,2048]{2,1,0:T(8,128)(2,1)S(1)}, bf16[2,128,2048]{2,1,0:T(8,128)(2,1)}, u32[]{:S(2)}) copy-start(bf16[2,128,2048]{2,1,0:T(8,128)(2,1)} %param.21) | copy-start | bytes 3145732
  204.3 160.8 %all-gather.16.cloned.1.call-start = ((), (), s32[]{:S(2)}) async-start(), calls=%async_computation.13 | async-start | bytes 5242880 | tf_op jit(solution)/shard_map/all_gather | solution.py:196
  283.7 172.0 %all-gather.18.cloned.1.call-start = ((), (), s32[]{:S(2)}) async-start(), calls=%async_computation.14 | async-start | bytes 18874368 | tf_op jit(solution)/shard_map/all_gather | solution.py:142
  287.9 3.1 copy-start.3
  290.2 247.8 %all-gather.22.cloned.1.call-start = ((), (), s32[]{:S(2)}) async-start(), calls=%async_computation.17 | async-start | bytes 5242880 | tf_op jit(solution)/shard_map/all_gather | solution.py:145
  290.9 303.9 %all-gather.20.cloned.1.call-start = ((), (), s32[]{:S(2)}) async-start(), calls=%async_computation.15 | async-start | bytes 9437184 | tf_op jit(solution)/shard_map/all_gather | solution.py:146
  292.1 425.2 %reduce-scatter.16.cloned.1.call-start = ((), (), s32[]{:S(2)}) async-start(), calls=%async_computation.18 | async-start | bytes 5242880 | tf_op jit(solution)/shard_map/reduce_scatter | solution.py:184
  640.3 77.0 %copy-start.1 = (bf16[2,128,2048]{2,1,0:T(8,128)(2,1)S(1)}, bf16[2,128,2048]{2,1,0:T(8,128)(2,1)}, u32[]{:S(2)}) copy-start(bf16[2,128,2048]{2,1,0:T(8,128)(2,1)} %reduce-scatter.12.cloned.1.call-done) | copy-start | bytes 3145732
  640.3 79.0 %copy-start.2 = (bf16[2,128,2048]{2,1,0:T(8,128)(2,1)S(1)}, bf16[2,128,2048]{2,1,0:T(8,128)(2,1)}, u32[]{:S(2)}) copy-start(bf16[2,128,2048]{2,1,0:T(8,128)(2,1)} %param.23) | copy-start | bytes 3145732
  640.4 163.6 %all-gather.24.cloned.1.call-start = ((), (), s32[]{:S(2)}) async-start(), calls=%async_computation.19 | async-start | bytes 5242880 | tf_op jit(solution)/shard_map/all_gather | solution.py:226
  722.6 255.0 %reduce-scatter.18.cloned.1.call-start = ((), (), s32[]{:S(2)}) async-start(), calls=%async_computation.20 | async-start | bytes 5242880 | tf_op jit(solution)/shard_map/reduce_scatter | solution.py:184
  877.9 10.4 copy-start.5
  877.9 10.4 copy-start.7
  877.9 10.3 copy-start.12
  888.2 1.6 copy-start.16
  889.9 7.2 copy-start.8
  897.1 5.1 copy-start.13
  902.2 150.6 %reduce-scatter.26.cloned.1.call-start = ((), (), s32[]{:S(2)}) async-start(), calls=%async_computation.24 | async-start | bytes 9437184 | tf_op jit(solution)/shard_map/reduce_scatter | solution.py:215
  916.8 180.4 %reduce-scatter.22.cloned.1.call-start = ((), (), s32[]{:S(2)}) async-start(), calls=%async_computation.22 | async-start | bytes 2359296 | tf_op jit(solution)/shard_map/reduce_scatter | solution.py:258
  923.0 223.5 %reduce-scatter.20.cloned.1.call-start = ((), (), s32[]{:S(2)}) async-start(), calls=%async_computation.21 | async-start | bytes 3538944 | tf_op jit(solution)/shard_map/reduce_scatter | solution.py:255
  931.0 294.5 %reduce-scatter.14.cloned.1.call-start = ((), (), s32[]{:S(2)}) async-start(), calls=%async_computation.16 | async-start | bytes 5242880 | tf_op jit(solution)/shard_map/reduce_scatter | solution.py:184
  945.1 32.5 %copy-start.20 = (f32[1,2048]{1,0:T(1,128)S(1)}, f32[1,2048]{1,0:T(1,128)}, u32[]{:S(2)}) copy-start(f32[1,2048]{1,0:T(1,128)} %copy-done.19) | copy-start | bytes 24580
  945.1 32.5 %copy-start.23 = (f32[2,128]{1,0:T(2,128)S(1)}, f32[2,128]{1,0:T(2,128)}, u32[]{:S(2)}) copy-start(f32[2,128]{1,0:T(2,128)} %copy-done.22) | copy-start | bytes 3076
  945.1 420.6 %reduce-scatter.28.cloned.1.call-start = ((), (), s32[]{:S(2)}) async-start(), calls=%async_computation.25 | async-start | bytes 1081344
  981.0 500.8 %reduce-scatter.24.cloned.1.call-start = ((), (), s32[]{:S(2)}) async-start(), calls=%async_computation.23 | async-start | bytes 18874368 | tf_op jit(solution)/shard_map/reduce_scatter | solution.py:219
  1097.2 9.0 copy-start.15
  1150.0 216.7 %copy-start.26 = (f32[64]{0:T(128)S(1)}, f32[64]{0:T(128)}, u32[]{:S(2)}) copy-start(f32[64]{0:T(128)} %param.27) | copy-start | bytes 772
  1150.0 216.7 %copy-start.28 = (f32[64]{0:T(128)S(1)}, f32[64]{0:T(128)}, u32[]{:S(2)}) copy-start(f32[64]{0:T(128)} %param.33) | copy-start | bytes 772
  1150.0 216.7 %copy-start.29 = (f32[64]{0:T(128)S(1)}, f32[64]{0:T(128)}, u32[]{:S(2)}) copy-start(f32[64]{0:T(128)} %param.39) | copy-start | bytes 772
  1150.0 217.3 %copy-start.27 = (f32[64]{0:T(128)S(1)}, f32[64]{0:T(128)}, u32[]{:S(2)}) copy-start(f32[64]{0:T(128)} %param.24) | copy-start | bytes 772
  1150.1 217.3 %copy-start.30 = (f32[64]{0:T(128)S(1)}, f32[64]{0:T(128)}, u32[]{:S(2)}) copy-start(f32[64]{0:T(128)} %param.30) | copy-start | bytes 772
  1150.1 217.3 %copy-start.31 = (f32[64]{0:T(128)S(1)}, f32[64]{0:T(128)}, u32[]{:S(2)}) copy-start(f32[64]{0:T(128)} %param.36) | copy-start | bytes 772
  1366.7 140.5 %copy-start.24 = (f32[64,1]{0,1:T(1,128)}, f32[64,1]{0,1:T(1,128)S(1)}, u32[]{:S(2)}) copy-start(f32[64,1]{0,1:T(1,128)S(1)} %copy.120) | copy-start | bytes 772
  1366.8 140.4 %copy-start.25 = (f32[64,1]{0,1:T(1,128)}, f32[64,1]{0,1:T(1,128)S(1)}, u32[]{:S(2)}) copy-start(f32[64,1]{0,1:T(1,128)S(1)} %copy.119) | copy-start | bytes 772
Sparse Core Ops, SparseCore 0:
  10.5 34.9 all-gather.11
  84.1 76.9 all-gather.9
  163.6 26.5 all-gather.13
  204.4 74.9 reduce-scatter.11
  283.8 81.2 all-gather.15
  367.4 88.2 all-gather.17
  457.2 80.7 all-gather.21
  540.4 54.3 all-gather.19
  640.5 76.7 reduce-scatter.15
  722.7 81.2 all-gather.23
  902.3 75.2 reduce-scatter.17
  980.9 71.7 reduce-scatter.25
  1056.1 41.0 reduce-scatter.21
  1100.4 46.0 reduce-scatter.19
  1148.6 76.7 reduce-scatter.13
  1228.1 137.5 reduce-scatter.27
  1369.1 112.5 reduce-scatter.23
where the time goes:
time: 1520 us; the launch traced here: 1510 us
  waiting for transfers between devices  1050 us (69%)
  matrix products  248 us (16%)
  other arithmetic  81.3 us (5%)
  blocking collectives  69.8 us (5%)
  local copies, waits for them, and re-layouts  43.9 us (3%)
    reduce_scatter x4, waiting for transfers between devices, to_local(): lax.psum_scatter(part.astype(jnp.bfloat16).reshape(seqs_here, full_len, w...  260 us
    unnamed x18, waiting for transfers between devices  136 us
    reduce_scatter x1, waiting for transfers between devices, per_device(): lax.psum_scatter(gate_up_term.astype(jnp.bfloat16), 'dp', scatter_dimensi...  114 us
    all_gather x1, waiting for transfers between devices, per_device(): lax.all_gather(gate_up_weight.astype(jnp.bfloat16).reshape(-1, 2 * unit_c...  90.6 us
    all_gather x1, waiting for transfers between devices, per_device(): lax.all_gather(d_resid.astype(jnp.bfloat16).reshape(seqs_here, local_len,...  81.3 us
    all_gather x1, waiting for transfers between devices, per_device(): lax.all_gather(normed_two_here.reshape(seqs_here, local_len, width), 'seq...  72.9 us
    all_gather x1, waiting for transfers between devices, per_device(): lax.all_gather(normed_here.reshape(seqs_here, local_len, width), 'seq', a...  70 us
    all_gather x1, blocking collectives, per_device(): gain_block = lax.all_gather(gain_pair, ('dp', 'seq'), axis=1, tiled=True)  69.8 us
  transfers between devices with their start and end apart: 17, of which 15 were waited for; matrix products, arithmetic and copies ran while one was open for 12% of the time, Pallas kernels for 0%

commit v1 on v0

--- a/solution.py
+++ b/solution.py
@@ -15,6 +15,18 @@
 adam_eps = 1e-08
 step_count = 10.0
 masked_score = -1e30
+
+
+def gather_by_bits(x, axis, dim):
+    ways, here = (lax.axis_size(axis), lax.axis_index(axis))
+    grown, reach = (x, 1)
+    while reach < ways:
+        theirs = lax.ppermute(grown, axis, [(d, d ^ reach) for d in range(ways)])
+        mine_first = jnp.concatenate([grown, theirs], axis=dim)
+        theirs_first = jnp.concatenate([theirs, grown], axis=dim)
+        grown = jnp.where(here & reach == 0, mine_first, theirs_first)
+        reach = 2 * reach
+    return grown
 
 
 def segment_positions(segments):
@@ -139,8 +151,8 @@
     ).reshape(total_rows, width)
     qkv_cols = lax.all_gather(qkv_weight.astype(jnp.bfloat16), "dp", axis=0, tiled=True)
     out_rows = lax.all_gather(out_weight.astype(jnp.bfloat16), "dp", axis=1, tiled=True)
-    gate_up_cols = lax.all_gather(
-        gate_up_weight.astype(jnp.bfloat16).reshape(-1, 2 * unit_count), "dp", axis=0, tiled=True
+    gate_up_cols = gather_by_bits(
+        gate_up_weight.astype(jnp.bfloat16).reshape(-1, 2 * unit_count), "dp", 0
     )
     cot_all = lax.all_gather(cotangent, "seq", axis=1, tiled=True)
     down_rows = lax.all_gather(down_weight.astype(jnp.bfloat16), "dp", axis=1, tiled=True)

time: 1520 us -> 1570 us (1.033)
  waiting for transfers between devices: 1050 us -> 1090 us
  other arithmetic: 81.3 us -> 97.1 us
    ppermute x0 -> x3, waiting for transfers between devices: none -> 309 us  [gather_by_bits(): theirs = lax.ppermute(grown, axis, [(d, d ^ reach) for d in range(ways)])]
    all_gather x1 -> x0, waiting for transfers between devices: 90.6 us -> none  [per_device(): lax.all_gather(gate_up_weight.astype(jnp.bfloat16).reshape(-1, 2 * unit_c...]
    all_gather x1, waiting for transfers between devices: 72.9 us -> 0.01 us  [per_device(): lax.all_gather(normed_two_here.reshape(seqs_here, local_len, width), 'seq...]
    all_gather x1, waiting for transfers between devices: 58.4 us -> 0.01 us  [per_device(): cot_all = lax.all_gather(cotangent, 'seq', axis=1, tiled=True)]
    all_gather x1, waiting for transfers between devices: 56.8 us -> 0.01 us  [per_device(): lax.all_gather(down_weight.astype(jnp.bfloat16), 'dp', axis=1, tiled=True)]
    select_n x0 -> x2, other arithmetic: none -> 15.8 us  [gather_by_bits(): grown = jnp.where(here & reach == 0, mine_first, theirs_first)]
    unnamed x18 -> x17, waiting for transfers between devices: 136 us -> 136 us
  transfers between devices with their start and end apart: 17 -> 19, of which waited for: 15 -> 14; matrix products, arithmetic and copies ran while one was open for 12% -> 13% of each run, Pallas kernels for 0% -> 0%
where the time goes in v1:
time: 1570 us
  waiting for transfers between devices  1090 us (69%)
  matrix products  252 us (16%)
  other arithmetic  97.1 us (6%)
  blocking collectives  69.8 us (4%)
  local copies, waits for them, and re-layouts  42.7 us (3%)
    ppermute x3, waiting for transfers between devices, gather_by_bits(): theirs = lax.ppermute(grown, axis, [(d, d ^ reach) for d in range(ways)])  309 us
    reduce_scatter x4, waiting for transfers between devices, to_local(): lax.psum_scatter(part.astype(jnp.bfloat16).reshape(seqs_here, full_len, w...  260 us
    unnamed x17, waiting for transfers between devices  136 us
    reduce_scatter x1, waiting for transfers between devices, per_device(): lax.psum_scatter(gate_up_term.astype(jnp.bfloat16), 'dp', scatter_dimensi...  114 us
    all_gather x1, waiting for transfers between devices, per_device(): lax.all_gather(d_resid.astype(jnp.bfloat16).reshape(seqs_here, local_len,...  81.3 us
    all_gather x1, waiting for transfers between devices, per_device(): lax.all_gather(normed_here.reshape(seqs_here, local_len, width), 'seq', a...  70 us
    all_gather x1, blocking collectives, per_device(): gain_block = lax.all_gather(gain_pair, ('dp', 'seq'), axis=1, tiled=True)  69.8 us
    dot_general x4, matrix products, times_transpose(): lax.dot_general(left, right, (((1,), (1,)), ((), ())), preferred_element_...  58.3 us
  transfers between devices with their start and end apart: 19, of which 14 were waited for; matrix products, arithmetic and copies ran while one was open for 13% of the time, Pallas kernels for 0%

profile of v1, /device:TPU:0, one launch (start us, length us, event | category | flops | bytes accessed | tf_op | source)
XLA Modules:
  0.0 1566.0 jit_solution(11589303006721674715)
XLA Ops:
  7.3 2.0 convert_element_type.162
  10.0 69.8 %all-gather = bf16[32,64,2]{1,2,0:T(2,128)(2,1)S(1)} all-gather(bf16[1,64,2]{1,2,0:T(2,128)(2,1)S(1)} %maximum_bitcast_fusion.4), channel_id=1, replica_groups=mesh['dp'=8,'seq'=4] {'dp','seq'}, dimensions={0}, use_global_device_ids=true | all-gather | bytes 8448 | tf_op jit(solution)/shard_map/all_gather | solution.py:144
  79.9 1.5 fusion.33
  81.5 2.5 fusion.30
  86.3 4.8 copy.86
  91.1 70.0 %all-gather.9.cloned.1.call-done = bf16[2,512,2048]{2,1,0:T(8,128)(2,1)} async-done(((bf16[2,128,2048]{2,1,0:T(8,128)(2,1)}), bf16[2,512,2048]{2,1,0:T(8,128)(2,1)}) %all-gather.9.cloned.1.call-update) | async-done | bytes 4194320 | tf_op jit(solution)/shard_map/all_gather | solution.py:149
  161.2 6.3 fusion.9
  169.2 7.4 fusion.5
  176.6 9.6 exponential_reduce_fusion
  186.2 10.3 fusion.36
  197.9 6.4 convolution_convert_fusion.2
  204.8 74.6 %reduce-scatter.12.cloned.1.call-done = bf16[2,128,2048]{2,1,0:T(8,128)(2,1)} async-done(((bf16[2,512,2048]{2,1,0:T(8,128)(2,1)}), bf16[2,128,2048]{2,1,0:T(8,128)(2,1)}) %reduce-scatter.12.cloned.1.call-update) | async-done | bytes 1048592 | tf_op jit(solution)/shard_map/reduce_scatter | solution.py:196
  279.4 1.6 multiply_reduce_fusion
  281.0 2.6 multiply_convert_fusion.3
  284.3 4.2 convert_element_type.174
  289.5 4.3 collective-permute-done
  293.7 4.8 maximum_select_fusion.2
  298.6 1.5 collective-permute-start.1
  301.2 90.3 %collective-permute-done.1 = bf16[512,4096]{1,0:T(8,128)(2,1)} collective-permute-done((bf16[512,4096]{1,0:T(8,128)(2,1)}, bf16[512,4096]{1,0:T(8,128)(2,1)}, u32[]{:S(2)}, u32[]{:S(2)}) %collective-permute-start.1) | collective-permute-done | bytes 4194336 | tf_op jit(solution)/shard_map/ppermute | solution.py:24
  391.5 11.0 maximum_select_fusion.1
  402.5 1.5 collective-permute-start.2
  404.0 214.2 %collective-permute-done.2 = bf16[1024,4096]{1,0:T(8,128)(2,1)} collective-permute-done((bf16[1024,4096]{1,0:T(8,128)(2,1)}, bf16[1024,4096]{1,0:T(8,128)(2,1)}, u32[]{:S(2)}, u32[]{:S(2)}) %collective-permute-start.2) | collective-permute-done | bytes 8388640 | tf_op jit(solution)/shard_map/ppermute | solution.py:24
  618.2 25.4 %fusion.19 = f32[1024,4096]{1,0:T(8,128)} fusion(bf16[1024,2048]{1,0:T(8,128)(2,1)} %bitcast.220, bf16[1024,4096]{1,0:T(8,128)(2,1)} %collective-permute-done.2, bf16[1024,4096]{1,0:T(8,128)(2,1)} %maximum_select_fusion.1, pred[]{:T(512)S(6)} %eq.29), kind=kOutput, calls=%fused_computation.47 | convolution fusion | flops 17255366656 | bytes 37748736 | tf_op jit(solution)/shard_map/dot_general | solution.py:211
  643.6 21.8 %multiply_convert_fusion.1 = (bf16[1024,2048]{1,0:T(8,128)(2,1)}, bf16[1024,2048]{1,0:T(8,128)(2,1)}, bf16[1024,2048]{1,0:T(8,128)(2,1)}) fusion(f32[1024,4096]{1,0:T(8,128)} %fusion.19, bf16[1024,2048]{1,0:T(8,128)(2,1)} %bitcast.222, bf16[2048,2048]{1,0:T(8,128)(2,1)} %all-gather.17.cloned.1.call-done), kind=kOutput, calls=%fused_computation.17 | convolution fusion | flops 8621391872 | bytes 41943040 | tf_op jit(solution)/shard_map/dot_general | solution.py:105
  665.4 25.3 %fusion.11 = bf16[1024,2048]{1,0:T(8,128)(2,1)} fusion(bf16[1024,2048]{1,0:T(8,128)(2,1)} %get-tuple-element.129, bf16[1024,2048]{1,0:T(8,128)(2,1)} %get-tuple-element.128, bf16[1024,4096]{1,0:T(8,128)(2,1)} %collective-permute-done.2, bf16[1024,4096]{1,0:T(8,128)(2,1)} %maximum_select_fusion.1, pred[]{:T(512)S(6)} %eq.29), kind=kOutput, calls=%fused_computation.29 | convolution fusion | flops 17274241024 | bytes 29360128 | tf_op jit(solution)/shard_map/dot_general | solution.py:105
  690.8 77.4 %reduce-scatter.16.cloned.1.call-done = bf16[2,128,2048]{2,1,0:T(8,128)(2,1)} async-done(((bf16[2,512,2048]{2,1,0:T(8,128)(2,1)}), bf16[2,128,2048]{2,1,0:T(8,128)(2,1)}) %reduce-scatter.16.cloned.1.call-update) | async-done | bytes 1048592 | tf_op jit(solution)/shard_map/reduce_scatter | solution.py:196
  768.1 2.0 fusion.29
  770.2 3.2 fusion.39
  773.5 81.3 %all-gather.21.cloned.1.call-done = bf16[2,512,2048]{2,1,0:T(8,128)(2,1)} async-done(((bf16[2,128,2048]{2,1,0:T(8,128)(2,1)}), bf16[2,512,2048]{2,1,0:T(8,128)(2,1)}) %all-gather.21.cloned.1.call-update) | async-done | bytes 4194320 | tf_op jit(solution)/shard_map/all_gather | solution.py:238
  854.8 6.2 convolution_convert_fusion.7
  861.0 4.8 reshape.347
  865.8 4.0 copy.90
  869.9 9.6 fusion.43
  879.4 24.6 %fusion.18 = f32[2,2,64,4,512]{4,2,3,1,0:T(8,128)} fusion(f32[2,2,512,512,4]{3,2,4,1,0:T(8,128)} %fusion.43, f32[2,2,512,512,4]{3,2,4,1,0:T(8,128)} %get-tuple-element.148, f32[2,2,4,512]{3,2,1,0:T(4,128)S(1)} %bitcast.214, pred[2,512,512]{1,2,0:T(8,128)(4,1)} %copy-done.10, bf16[2,512,2,32]{1,3,2,0:T(8,128)(2,1)S(1)} %copy-done.22, ...), kind=kOutput, calls=%fused_computation.45 | convolution fusion | flops 583541248 | bytes 36470784 | tf_op jit(solution)/shard_map/sgjqk,skgd->sqgjd/dot_general | solution.py:250
  904.1 25.1 %fusion.37 = f32[2,512,2,64]{1,3,2,0:T(8,128)} fusion(f32[2,2,512,512,4]{3,2,4,1,0:T(8,128)} %fusion.43, f32[2,2,512,512,4]{3,2,4,1,0:T(8,128)} %get-tuple-element.148, f32[2,2,4,512]{3,2,1,0:T(4,128)S(1)} %bitcast.215, pred[2,512,512]{1,2,0:T(8,128)(4,1)} %copy-done.10, bf16[2,512,2,4,32]{1,4,3,2,0:T(8,128)(2,1)} %bitcast.200, ...), kind=kOutput, calls=%fused_computation.79 | convolution fusion | flops 585114112 | bytes 35684352 | tf_op jit(solution)/shard_map/sgjqk,sqgjd->skgd/dot_general | solution.py:251
  929.2 10.3 convolution_bitcast_fusion
  941.8 6.1 maximum_convert_fusion
  948.4 5.0 convolution_convert_fusion.3
  953.5 14.3 convert_bitcast_fusion
  967.8 6.3 convolution_convert_fusion.5
  974.2 7.9 convolution_convert_fusion.4
  982.2 14.1 convolution_convert_fusion.1
  996.3 32.6 %reduce-scatter.18.cloned.1.call-done = bf16[2,128,2048]{2,1,0:T(8,128)(2,1)} async-done(((bf16[2,512,2048]{2,1,0:T(8,128)(2,1)}), bf16[2,128,2048]{2,1,0:T(8,128)(2,1)}) %reduce-scatter.18.cloned.1.call-update) | async-done | bytes 1048592 | tf_op jit(solution)/shard_map/reduce_scatter | solution.py:196
  1028.9 1.9 fusion.32
  1032.3 25.4 %convolution_convert_fusion = bf16[2048,4096]{1,0:T(8,128)(2,1)} fusion(bf16[1024,2048]{1,0:T(8,128)(2,1)} %bitcast.221, bf16[1024,2048]{1,0:T(8,128)(2,1)} %get-tuple-element.129, bf16[1024,2048]{1,0:T(8,128)(2,1)} %get-tuple-element.128), kind=kOutput, calls=%fused_computation.10 | convolution fusion | flops 17205035008 | bytes 29360128 | tf_op jit(solution)/shard_map/dot_general | solution.py:99
  1057.7 2.2 copy.101
  1059.9 2.0 copy.98
  1062.0 2.0 copy.99
  1064.0 40.2 %reduce-scatter.26.cloned.1.call-done = bf16[256,2048]{0,1:T(8,128)(2,1)} async-done(((bf16[2048,2048]{0,1:T(8,128)(2,1)}), bf16[256,2048]{0,1:T(8,128)(2,1)}) %reduce-scatter.26.cloned.1.call-update) | async-done | bytes 1048592 | tf_op jit(solution)/shard_map/reduce_scatter | solution.py:227
  1104.2 6.9 multiply_subtract_fusion.1
  1111.1 37.4 %reduce-scatter.22.cloned.1.call-done = bf16[256,512]{1,0:T(8,128)(2,1)} async-done(((bf16[2048,512]{1,0:T(8,128)(2,1)}), bf16[256,512]{1,0:T(8,128)(2,1)}) %reduce-scatter.22.cloned.1.call-update) | async-done | bytes 262160 | tf_op jit(solution)/shard_map/reduce_scatter | solution.py:270
  1148.5 2.9 multiply_subtract_fusion.4
  1151.4 2.0 copy.103
  1153.4 2.0 copy.104
  1155.4 2.0 copy.105
  1158.3 2.1 copy.102
  1160.4 37.6 %reduce-scatter.20.cloned.1.call-done = bf16[256,768]{1,0:T(8,128)(2,1)} async-done(((bf16[2048,768]{1,0:T(8,128)(2,1)}), bf16[256,768]{1,0:T(8,128)(2,1)}) %reduce-scatter.20.cloned.1.call-update) | async-done | bytes 393232 | tf_op jit(solution)/shard_map/reduce_scatter | solution.py:267
  1197.9 3.5 multiply_subtract_fusion.3
  1201.5 75.4 %reduce-scatter.14.cloned.1.call-done = bf16[2,128,2048]{2,1,0:T(8,128)(2,1)} async-done(((bf16[2,512,2048]{2,1,0:T(8,128)(2,1)}), bf16[2,128,2048]{2,1,0:T(8,128)(2,1)}) %reduce-scatter.14.cloned.1.call-update) | async-done | bytes 1048592 | tf_op jit(solution)/shard_map/reduce_scatter | solution.py:196
  1276.9 4.9 fusion.25
  1281.8 135.4 %reduce-scatter.28.cloned.1.call-done = f32[64,2]{1,0:T(8,128)} async-done(((f32[2048,2]{1,0:T(8,128)}), f32[64,2]{1,0:T(8,128)}) %reduce-scatter.28.cloned.1.call-update) | async-done | bytes 528
  1419.4 114.1 %reduce-scatter.24.cloned.1.call-done = bf16[256,4096]{1,0:T(8,128)(2,1)} async-done(((bf16[2048,4096]{1,0:T(8,128)(2,1)}), bf16[256,4096]{1,0:T(8,128)(2,1)}) %reduce-scatter.24.cloned.1.call-update) | async-done | bytes 2097168 | tf_op jit(solution)/shard_map/reduce_scatter | solution.py:231
  1533.5 6.6 reshape.336
  1540.1 18.9 %multiply_subtract_fusion = (f32[256,2,2048]{2,1,0:T(2,128)}, f32[256,2,2048]{2,1,0:T(2,128)}, f32[256,2,2048]{2,1,0:T(2,128)}) fusion(f32[256,2,2048]{2,1,0:T(2,128)} %param.28, f32[256,2,2048]{2,1,0:T(2,128)} %reshape.336, f32[256,2,2048]{2,1,0:T(2,128)} %param.34, f32[256,2,2048]{2,1,0:T(2,128)} %param.40), kind=kLoop, calls=%fused_computation.27 | loop fusion | flops 15728640 | bytes 29360128 | tf_op jit(solution)/shard_map/sub | solution.py:92
  (151 shorter events, 16.9 us)
Async XLA Ops:
  7.2 76.8 %copy-start.11 = (f32[512,256]{1,0:T(8,128)S(1)}, f32[512,256]{1,0:T(8,128)}, u32[]{:S(2)}) copy-start(f32[512,256]{1,0:T(8,128)} %param.26) | copy-start | bytes 1572868
  7.2 77.8 %copy-start.25 = (s32[2,512]{1,0:T(2,128)S(1)}, s32[2,512]{1,0:T(2,128)}, u32[]{:S(2)}) copy-start(s32[2,512]{1,0:T(2,128)} %param.22) | copy-start | bytes 12292
  7.2 79.1 %all-gather.11.cloned.1.call-start = ((), (), s32[]{:S(2)}) async-start(), calls=%async_computation.10 | async-start | bytes 3538944 | tf_op jit(solution)/shard_map/all_gather | solution.py:152
  9.3 151.9 %all-gather.9.cloned.1.call-start = ((), (), s32[]{:S(2)}) async-start(), calls=%async_computation.9 | async-start | bytes 5242880 | tf_op jit(solution)/shard_map/all_gather | solution.py:149
  81.4 3.8 copy-start.26
  81.5 3.8 copy-start.23
  84.0 113.9 %all-gather.13.cloned.1.call-start = ((), (), s32[]{:S(2)}) async-start(), calls=%async_computation.11 | async-start | bytes 2359296 | tf_op jit(solution)/shard_map/all_gather | solution.py:153
  84.8 194.6 %reduce-scatter.12.cloned.1.call-start = ((), (), s32[]{:S(2)}) async-start(), calls=%async_computation.12 | async-start | bytes 5242880 | tf_op jit(solution)/shard_map/reduce_scatter | solution.py:196
  85.7 100.5 %copy-start.10 = (pred[2,512,512]{1,2,0:T(8,128)(4,1)}, pred[2,512,512]{1,2,0:T(8,128)(4,1)S(1)}, u32[]{:S(2)}) copy-start(pred[2,512,512]{1,2,0:T(8,128)(4,1)S(1)} %compare_and_fusion) | copy-start | bytes 1572868
  86.3 81.6 %copy-start.4 = (f32[2,512,32]{1,2,0:T(8,128)}, f32[2,512,32]{1,2,0:T(8,128)S(1)}, u32[]{:S(2)}) copy-start(f32[2,512,32]{1,2,0:T(8,128)S(1)} %get-tuple-element.145) | copy-start | bytes 393220
  86.3 81.6 %copy-start.6 = (f32[2,512,32]{1,2,0:T(8,128)}, f32[2,512,32]{1,2,0:T(8,128)S(1)}, u32[]{:S(2)}) copy-start(f32[2,512,32]{1,2,0:T(8,128)S(1)} %get-tuple-element.146) | copy-start | bytes 393220
  167.5 1.7 copy-start.9
  167.6 8.9 copy-start.19
  167.7 8.9 copy-start.21
  169.1 7.4 copy-start.17
  169.2 7.4 copy-start.18
  197.9 6.4 copy-start.14
  204.3 75.1 %copy-start = (bf16[2,128,2048]{2,1,0:T(8,128)(2,1)S(1)}, bf16[2,128,2048]{2,1,0:T(8,128)(2,1)}, u32[]{:S(2)}) copy-start(bf16[2,128,2048]{2,1,0:T(8,128)(2,1)} %param.21) | copy-start | bytes 3145732
  204.3 413.9 %all-gather.15.cloned.1.call-start = ((), (), s32[]{:S(2)}) async-start(), calls=%async_computation.13 | async-start | bytes 5242880 | tf_op jit(solution)/shard_map/all_gather | solution.py:208
  283.6 360.0 %all-gather.19.cloned.1.call-start = ((), (), s32[]{:S(2)}) async-start(), calls=%async_computation.16 | async-start | bytes 5242880 | tf_op jit(solution)/shard_map/all_gather | solution.py:157
  284.2 359.4 %all-gather.17.cloned.1.call-start = ((), (), s32[]{:S(2)}) async-start(), calls=%async_computation.14 | async-start | bytes 9437184 | tf_op jit(solution)/shard_map/all_gather | solution.py:158
  289.4 4.4 collective-permute-start
  289.5 10.6 copy-start.3
  298.6 92.9 %collective-permute-start.1 = (bf16[512,4096]{1,0:T(8,128)(2,1)}, bf16[512,4096]{1,0:T(8,128)(2,1)}, u32[]{:S(2)}, u32[]{:S(2)}) collective-permute-start(bf16[512,4096]{1,0:T(8,128)(2,1)} %maximum_select_fusion.2), channel_id=1, source_target_pairs={{0,8},{4,12},{8,0},{12,4},{16,24},{20,28},{24,16},{28,20},{1,9},{5... | collective-permute-start | bytes 12582920 | tf_op jit(solution)/shard_map/ppermute | solution.py:24
  301.2 466.9 %reduce-scatter.16.cloned.1.call-start = ((), (), s32[]{:S(2)}) async-start(), calls=%async_computation.17 | async-start | bytes 5242880 | tf_op jit(solution)/shard_map/reduce_scatter | solution.py:196
  402.5 215.7 %collective-permute-start.2 = (bf16[1024,4096]{1,0:T(8,128)(2,1)}, bf16[1024,4096]{1,0:T(8,128)(2,1)}, u32[]{:S(2)}, u32[]{:S(2)}) collective-permute-start(bf16[1024,4096]{1,0:T(8,128)(2,1)} %maximum_select_fusion.1), channel_id=1, source_target_pairs={{0,16},{4,20},{8,24},{12,28},{16,0},{20,4},{24,8},{28,12},{1,17},{... | collective-permute-start | bytes 25165832 | tf_op jit(solution)/shard_map/ppermute | solution.py:24
  690.7 77.4 %copy-start.1 = (bf16[2,128,2048]{2,1,0:T(8,128)(2,1)S(1)}, bf16[2,128,2048]{2,1,0:T(8,128)(2,1)}, u32[]{:S(2)}) copy-start(bf16[2,128,2048]{2,1,0:T(8,128)(2,1)} %reduce-scatter.12.cloned.1.call-done) | copy-start | bytes 3145732
  690.7 79.5 %copy-start.2 = (bf16[2,128,2048]{2,1,0:T(8,128)(2,1)S(1)}, bf16[2,128,2048]{2,1,0:T(8,128)(2,1)}, u32[]{:S(2)}) copy-start(bf16[2,128,2048]{2,1,0:T(8,128)(2,1)} %param.23) | copy-start | bytes 3145732
  690.7 164.1 %all-gather.21.cloned.1.call-start = ((), (), s32[]{:S(2)}) async-start(), calls=%async_computation.18 | async-start | bytes 5242880 | tf_op jit(solution)/shard_map/all_gather | solution.py:238
  773.4 255.5 %reduce-scatter.18.cloned.1.call-start = ((), (), s32[]{:S(2)}) async-start(), calls=%async_computation.19 | async-start | bytes 5242880 | tf_op jit(solution)/shard_map/reduce_scatter | solution.py:196
  869.9 9.6 copy-start.20
  869.9 9.6 copy-start.22
  929.2 10.4 copy-start.5
  929.2 10.4 copy-start.7
  929.2 10.4 copy-start.12
  939.5 1.6 copy-start.16
  941.2 7.2 copy-start.8
  948.4 5.1 copy-start.13
  953.4 150.7 %reduce-scatter.26.cloned.1.call-start = ((), (), s32[]{:S(2)}) async-start(), calls=%async_computation.23 | async-start | bytes 9437184 | tf_op jit(solution)/shard_map/reduce_scatter | solution.py:227
  967.8 180.7 %reduce-scatter.22.cloned.1.call-start = ((), (), s32[]{:S(2)}) async-start(), calls=%async_computation.21 | async-start | bytes 2359296 | tf_op jit(solution)/shard_map/reduce_scatter | solution.py:270
  974.1 223.8 %reduce-scatter.20.cloned.1.call-start = ((), (), s32[]{:S(2)}) async-start(), calls=%async_computation.20 | async-start | bytes 3538944 | tf_op jit(solution)/shard_map/reduce_scatter | solution.py:267
  982.1 294.8 %reduce-scatter.14.cloned.1.call-start = ((), (), s32[]{:S(2)}) async-start(), calls=%async_computation.15 | async-start | bytes 5242880 | tf_op jit(solution)/shard_map/reduce_scatter | solution.py:196
  996.3 32.6 %copy-start.24 = (f32[1,2048]{1,0:T(1,128)S(1)}, f32[1,2048]{1,0:T(1,128)}, u32[]{:S(2)}) copy-start(f32[1,2048]{1,0:T(1,128)} %copy-done.23) | copy-start | bytes 24580
  996.3 32.6 %copy-start.27 = (f32[2,128]{1,0:T(2,128)S(1)}, f32[2,128]{1,0:T(2,128)}, u32[]{:S(2)}) copy-start(f32[2,128]{1,0:T(2,128)} %copy-done.26) | copy-start | bytes 3076
  996.3 420.9 %reduce-scatter.28.cloned.1.call-start = ((), (), s32[]{:S(2)}) async-start(), calls=%async_computation.24 | async-start | bytes 1081344
  1032.2 501.3 %reduce-scatter.24.cloned.1.call-start = ((), (), s32[]{:S(2)}) async-start(), calls=%async_computation.22 | async-start | bytes 18874368 | tf_op jit(solution)/shard_map/reduce_scatter | solution.py:231
  1148.5 9.0 copy-start.15
  1201.5 216.8 %copy-start.30 = (f32[64]{0:T(128)S(1)}, f32[64]{0:T(128)}, u32[]{:S(2)}) copy-start(f32[64]{0:T(128)} %param.27) | copy-start | bytes 772
  1201.5 216.8 %copy-start.32 = (f32[64]{0:T(128)S(1)}, f32[64]{0:T(128)}, u32[]{:S(2)}) copy-start(f32[64]{0:T(128)} %param.33) | copy-start | bytes 772
  1201.5 216.8 %copy-start.33 = (f32[64]{0:T(128)S(1)}, f32[64]{0:T(128)}, u32[]{:S(2)}) copy-start(f32[64]{0:T(128)} %param.39) | copy-start | bytes 772
  1201.5 217.3 %copy-start.31 = (f32[64]{0:T(128)S(1)}, f32[64]{0:T(128)}, u32[]{:S(2)}) copy-start(f32[64]{0:T(128)} %param.24) | copy-start | bytes 772
  1201.5 217.3 %copy-start.34 = (f32[64]{0:T(128)S(1)}, f32[64]{0:T(128)}, u32[]{:S(2)}) copy-start(f32[64]{0:T(128)} %param.30) | copy-start | bytes 772
  1201.5 217.3 %copy-start.35 = (f32[64]{0:T(128)S(1)}, f32[64]{0:T(128)}, u32[]{:S(2)}) copy-start(f32[64]{0:T(128)} %param.36) | copy-start | bytes 772
  1418.2 140.8 %copy-start.28 = (f32[64,1]{0,1:T(1,128)}, f32[64,1]{0,1:T(1,128)S(1)}, u32[]{:S(2)}) copy-start(f32[64,1]{0,1:T(1,128)S(1)} %copy.120) | copy-start | bytes 772
  1418.3 140.7 %copy-start.29 = (f32[64,1]{0,1:T(1,128)}, f32[64,1]{0,1:T(1,128)S(1)}, u32[]{:S(2)}) copy-start(f32[64,1]{0,1:T(1,128)S(1)} %copy.119) | copy-start | bytes 772
Sparse Core Ops, SparseCore 0:
  10.5 34.9 all-gather.10
  84.1 76.9 all-gather.8
  163.6 26.5 all-gather.12
  204.4 74.9 reduce-scatter.11
  283.8 81.2 all-gather.14
  366.5 79.2 all-gather.18
  448.2 88.2 all-gather.16
  690.8 77.2 reduce-scatter.15
  773.5 81.2 all-gather.20
  953.6 75.2 reduce-scatter.17
  1032.4 71.7 reduce-scatter.25
  1107.3 41.0 reduce-scatter.21
  1151.8 46.0 reduce-scatter.19
  1200.1 76.7 reduce-scatter.13
  1279.6 137.5 reduce-scatter.27
  1420.6 112.8 reduce-scatter.23
